TPU v7x, 32 devices: a whole 2x2x4 slice. The times are simulated.
32 devices in a mesh: wide: 8 (over y, x, core), narrow: 4 (over z).
Axes of the slice: x: 2, y: 2, z: 4, core: 2. Of those that a mesh axis runs over, the one named last changes fastest.
Arguments:
- momentum: float32 [9216, 9216], P('wide', 'narrow'), may hold values from -3 to 3
- gradient: bfloat16 [9216, 9216], P('wide', 'narrow'), may hold values from -48 to 48
- right_factor: float32 [512, 9216], P('wide', 'narrow'), may hold values from -6 to 6
Outputs:
- new_momentum: float32 [9216, 9216], P('wide', 'narrow')
- new_right: float32 [512, 9216], P('wide', 'narrow')
- update: bfloat16 [9216, 9216], P('wide', 'narrow')
All inputs are finite; a program needn't handle non-finite values.
Results may differ from a plain program's by a relative error of at most 0.001.
Values sent between devices are 32-bit elements; how exact they have to be, the bound alone decides.
No kernel may reach another device: no remote copies, remote signals or barrier semaphores. Data moves between devices by JAX's collectives and lax.ppermute only.
A program may use at most 128 MiB of HBM per device.

v0:
```python
import jax
import jax.numpy as jnp
from jax import lax
from jax.sharding import PartitionSpec as P

N_COLS = 9216
EPS = 1e-06
MU = 0.95


def orthonormal(projected, gram_matrix):
    factor_lower = jnp.linalg.cholesky(gram_matrix)
    return jax.scipy.linalg.solve_triangular(factor_lower, projected.T, lower=True).T


def matmul(left, right):
    return jnp.dot(left, right, preferred_element_type=jnp.float32, precision=lax.Precision.HIGHEST)


def per_device(momentum, gradient, right_factor):
    blended = momentum + gradient.astype(jnp.float32)
    partial_left = matmul(blended, lax.all_gather(right_factor, "wide", axis=0, tiled=True).T)
    projected = lax.psum(partial_left, "narrow")
    gram_matrix = lax.psum(matmul(projected.T, projected), "wide")
    left_basis = orthonormal(projected, gram_matrix)
    columns = left_basis
    right_block = lax.psum_scatter(
        matmul(columns.T, blended), "wide", scatter_dimension=0, tiled=True
    )
    squares = lax.psum(jnp.sum(right_block * right_block, axis=1), "narrow")
    root_mean = jnp.sqrt(squares / N_COLS + EPS)
    new_right = right_block / root_mean[:, None]
    pieces = (
        lax.all_gather(right_block, "wide", axis=0, tiled=True),
        lax.all_gather(root_mean, "wide", axis=0, tiled=True),
    )
    columns = left_basis
    normed = pieces[0] / pieces[1][:, None]
    feedback = matmul(columns, pieces[0])
    direction = matmul(columns, normed)
    new_momentum = blended - (1.0 - MU) * feedback
    return (new_momentum, new_right, direction.astype(jnp.bfloat16))


def solution(mesh):
    return jax.shard_map(
        per_device,
        mesh=mesh,
        in_specs=(P("wide", "narrow"), P("wide", "narrow"), P("wide", "narrow")),
        out_specs=(P("wide", "narrow"), P("wide", "narrow"), P("wide", "narrow")),
        check_vma=False,
    )
```

profile of v0, /device:TPU:0, one launch (start us, length us, event | category | flops | bytes accessed | tf_op | source)
XLA Modules:
  0.0 566.0 jit_solution(15770033689719844626)
XLA Ops:
  7.2 0.7 all-gather.3.cloned.1.call-update
  7.9 43.5 %all-gather.3.cloned.1.call-done = f32[512,2304]{1,0:T(8,128)} async-done(((f32[64,2304]{1,0:T(8,128)}), f32[512,2304]{1,0:T(8,128)}) %all-gather.3.cloned.1.call-update) | async-done | bytes 4718608 | tf_op jit(solution)/shard_map/all_gather | solution.py:22
  51.4 22.9 %fusion.3 = f32[1152,512]{1,0:T(8,128)} fusion(f32[512,2304]{1,0:T(8,128)} %all-gather.3.cloned.1.call-done, f32[1152,2304]{1,0:T(8,128)} %param.3, bf16[1152,2304]{1,0:T(8,128)(2,1)} %param.4), kind=kOutput, calls=%fused_computation.8 | convolution fusion | flops 16312762368 | bytes 23003136 | tf_op jit(solution)/shard_map/dot_general | solution.py:17
  74.3 0.0 all-reduce.7.cloned.1.call-start
  74.4 94.7 %all-reduce.5.cloned.1.call-done = f32[1152,512]{1,0:T(8,128)} async-done(((f32[1152,512]{1,0:T(8,128)}), f32[1152,512]{1,0:T(8,128)}) %all-reduce.5.cloned.1.call-update) | async-done | bytes 2359312 | tf_op jit(solution)/shard_map/psum | solution.py:23
  169.1 7.7 %fusion.40 = f32[512,512]{0,1:T(8,128)} fusion(f32[1152,512]{1,0:T(8,128)} %all-reduce.5.cloned.1.call-done), kind=kOutput, calls=%fused_computation.82 | convolution fusion | flops 3623878656 | bytes 3407872 | tf_op jit(solution)/shard_map/dot_general | solution.py:17
  176.8 0.3 reduce-scatter.2.cloned.1.call-start
  177.1 55.6 %all-reduce.7.cloned.1.call-done = f32[512,512]{0,1:T(8,128)} async-done(((f32[512,512]{0,1:T(8,128)}), f32[512,512]{0,1:T(8,128)}) %all-reduce.7.cloned.1.call-update) | async-done | bytes 1048592 | tf_op jit(solution)/shard_map/psum | solution.py:24
  232.7 1.6 copy.7
  234.3 0.2 fusion.13
  234.6 1.0 copy-done.5
  235.6 11.7 %cholesky.104 = f32[128,128]{1,0:T(8,128)S(1)} custom-call(f32[128,128]{1,0:T(8,128)S(1)} %cholesky.266), custom_call_target="Cholesky" | custom-call | tf_op jit(solution)/shard_map/jit(cholesky)/cholesky | solution.py:12
  247.3 9.8 %custom-call.31 = f32[1,128,128]{1,2,0:T(8,128)S(1)} custom-call(f32[1,128,128]{2,1,0:T(8,128)S(1)} %get-tuple-element.30), custom_call_target="InvertDiagBlocksLowerTriangular" | custom-call | tf_op jit(solution)/shard_map/jit(cholesky)/cholesky | solution.py:12
  257.1 0.1 cholesky.224
  257.2 1.2 constant_dynamic-update-slice_fusion.3
  258.5 1.3 convolution_subtract_fusion.3
  259.8 11.7 %cholesky.217 = f32[128,128]{1,0:T(8,128)S(1)} custom-call(f32[128,128]{1,0:T(8,128)S(1)} %cholesky.270), custom_call_target="Cholesky" | custom-call | tf_op jit(solution)/shard_map/jit(cholesky)/cholesky | solution.py:12
  271.5 10.2 %custom-call.32 = f32[1,128,128]{1,2,0:T(8,128)S(1)} custom-call(f32[1,128,128]{2,1,0:T(8,128)S(1)} %get-tuple-element.27), custom_call_target="InvertDiagBlocksLowerTriangular" | custom-call | tf_op jit(solution)/shard_map/jit(cholesky)/cholesky | solution.py:12
  281.7 0.3 convolution_dynamic-update-slice_fusion
  282.0 1.4 convolution_subtract_fusion.4
  283.4 0.6 cholesky.275
  284.1 13.2 %cholesky.238 = f32[128,128]{1,0:T(8,128)} custom-call(f32[128,128]{1,0:T(8,128)} %cholesky.275), custom_call_target="Cholesky" | custom-call | tf_op jit(solution)/shard_map/jit(cholesky)/cholesky | solution.py:12
  297.2 1.5 select_reduce_fusion.1
  298.7 0.7 compare_reduce_fusion.1
  299.4 11.3 %custom-call.33 = f32[1,128,128]{1,2,0:T(8,128)} custom-call(f32[1,128,128]{2,1,0:T(8,128)} %get-tuple-element.24), custom_call_target="InvertDiagBlocksLowerTriangular" | custom-call | tf_op jit(solution)/shard_map/jit(cholesky)/cholesky | solution.py:12
  310.7 1.0 convolution_dynamic-update-slice_fusion.1
  311.8 1.2 convolution_subtract_fusion.5
  313.0 11.7 %cholesky.255 = f32[128,128]{1,0:T(8,128)S(1)} custom-call(f32[128,128]{1,0:T(8,128)S(1)} %convolution_subtract_fusion.5), custom_call_target="Cholesky" | custom-call | tf_op jit(solution)/shard_map/jit(cholesky)/cholesky | solution.py:12
  324.7 0.6 compare_reduce_fusion
  325.4 0.6 compare_reduce_fusion.2
  328.5 1.3 select_select_fusion
  329.8 13.7 %while.1 = (s32[]{:T(128)}, f32[512,512]{1,0:T(8,128)}, s32[4,2]{0,1:T(2,128)S(1)}, f32[4,128,128]{2,1,0:T(8,128)}, s32[]{:T(128)}) while((s32[]{:T(128)}, f32[512,512]{1,0:T(8,128)}, s32[4,2]{0,1:T(2,128)S(1)}, f32[4,128,128]{2,1,0:T(8,128)}, s32[]{:T(128)}) %tuple.32), condition=%wide.while_cond, body=%wide.while_body.sunk | while | flops 2 | bytes 132205 | solution.py:13
  329.8 0.1 constant_dynamic-slice_fusion.2
  329.9 0.5 fusion.51
  330.4 2.8 bitcast_dynamic-update-slice_fusion.2
  333.2 0.1 constant_dynamic-slice_fusion.2
  333.3 0.5 fusion.51
  333.8 2.8 bitcast_dynamic-update-slice_fusion.2
  336.7 0.1 constant_dynamic-slice_fusion.2
  336.7 0.5 fusion.51
  337.3 2.8 bitcast_dynamic-update-slice_fusion.2
  340.1 0.1 constant_dynamic-slice_fusion.2
  340.2 0.5 fusion.51
  340.7 2.8 bitcast_dynamic-update-slice_fusion.2
  343.5 40.1 %custom-call.34 = f32[4,128,128]{1,2,0:T(8,128)S(1)} custom-call(f32[4,128,128]{2,1,0:T(8,128)} %get-tuple-element.10), custom_call_target="InvertDiagBlocksLowerTriangular" | custom-call | tf_op jit(solution)/shard_map/jit(_solve_triangular)/triangular_solve | solution.py:13
  383.6 0.7 fusion.14
  384.4 2.4 convolution_subtract_fusion.2
  386.8 1.6 fusion.27
  388.4 3.0 convolution_subtract_fusion.1
  391.5 0.7 fusion.25
  392.2 4.2 convolution_subtract_fusion
  396.5 0.7 fusion.24
  397.3 23.1 %fusion.2 = f32[512,2304]{1,0:T(8,128)} fusion(f32[1152,2304]{1,0:T(8,128)} %param.3, bf16[1152,2304]{1,0:T(8,128)(2,1)S(1)} %bitcast.55, f32[128,1152]{1,0:T(8,128)S(1)} %fusion.24, f32[128,1152]{1,0:T(8,128)S(1)} %fusion.25, f32[128,1152]{1,0:T(8,128)S(1)} %fusion.27, f32[128,1152]{1,0:T(8,128)S(1)} %fusion.14), kind=kOutput, calls=%fused_computation.7 | convolution fusion | flops 16314531840 | bytes 23003136 | tf_op jit(solution)/shard_map/dot_general | solution.py:17
  420.4 0.0 all-gather.5.cloned.1.call-start
  420.4 53.1 %reduce-scatter.2.cloned.1.call-done = f32[64,2304]{1,0:T(8,128)} async-done(((f32[512,2304]{1,0:T(8,128)}), f32[64,2304]{1,0:T(8,128)}) %reduce-scatter.2.cloned.1.call-update) | async-done | bytes 589840 | tf_op jit(solution)/shard_map/reduce_scatter | solution.py:27
  473.6 0.6 dynamic-slice.3
  474.8 1.2 multiply_reduce_fusion
  476.0 11.7 %psum.23 = f32[64]{0:T(128)S(1)} all-reduce(f32[64]{0:T(128)S(1)} %multiply_reduce_fusion), channel_id=1, replica_groups=mesh['wide'=8,'narrow'=4] {'narrow'}, use_global_device_ids=true, to_apply=%region_12.13 | all-reduce | flops 64 | bytes 512 | tf_op jit(solution)/shard_map/psum | solution.py:30
  487.7 0.1 fusion.38
  487.8 12.1 %all-reduce.1 = f32[512]{0:T(512)S(1)} all-reduce(f32[512]{0:T(512)S(1)} %get-tuple-element.31), channel_id=1, replica_groups=mesh['wide'=8,'narrow'=4] {'wide'}, use_global_device_ids=true, to_apply=%add.1 | all-reduce | flops 512 | bytes 4096
  499.9 2.0 broadcast_divide_fusion
  501.9 12.3 %all-gather.5.cloned.1.call-done = f32[512,2304]{1,0:T(8,128)} async-done(((f32[64,2304]{1,0:T(8,128)}), f32[512,2304]{1,0:T(8,128)}) %all-gather.5.cloned.1.call-update) | async-done | bytes 4718608 | tf_op jit(solution)/shard_map/all_gather | solution.py:34
  514.2 24.1 %fusion = f32[1152,2304]{1,0:T(8,128)} fusion(f32[512,2304]{1,0:T(8,128)} %all-gather.5.cloned.1.call-done, f32[1152,2304]{1,0:T(8,128)} %param.3, bf16[1152,2304]{1,0:T(8,128)(2,1)} %param.4, f32[128,1152]{1,0:T(8,128)S(1)} %fusion.24, f32[128,1152]{1,0:T(8,128)S(1)} %copy-done.2, f32[128,1152]{1,0:T(8,128)S(1)} %fusion.27, f32[128,1152]{1,0:T(8,128)S(1)} %fusion.14), kind=kOutput, calls=%fused_computation.3 | convolution fusion | flops 16319840256 | bytes 33619968 | tf_op jit(solution)/shard_map/dot_general | solution.py:17
  538.3 20.7 %convolution_convert_fusion = bf16[1152,2304]{1,0:T(8,128)(2,1)} fusion(f32[512,2304]{1,0:T(8,128)S(1)} %copy-done.3, f32[512]{0:T(512)S(1)} %all-reduce.1, f32[128,1152]{1,0:T(8,128)S(1)} %fusion.24, f32[128,1152]{1,0:T(8,128)S(1)} %copy-done.2, f32[128,1152]{1,0:T(8,128)S(1)} %fusion.27, f32[128,1152]{1,0:T(8,128)S(1)} %fusion.14), kind=kOutput, calls=%fused_computation.4 | convolution fusion | flops 16313057280 | bytes 12388352 | tf_op jit(solution)/shard_map/dot_general | solution.py:17
  (37 shorter events, 0.3 us)
Async XLA Ops:
  7.2 44.2 %all-gather.3.cloned.1.call-start = ((), (), s32[]{:S(2)}) async-start(), calls=%async_computation.1 | async-start | bytes 5308416 | tf_op jit(solution)/shard_map/all_gather | solution.py:22
  7.9 161.2 %all-reduce.5.cloned.1.call-start = ((), (), s32[]{:S(2)}) async-start(), calls=%async_computation.2 | async-start | bytes 4718592 | tf_op jit(solution)/shard_map/psum | solution.py:23
  74.3 158.4 %all-reduce.7.cloned.1.call-start = ((), (), s32[]{:S(2)}) async-start(), calls=%async_computation.3 | async-start | bytes 2097152 | tf_op jit(solution)/shard_map/psum | solution.py:24
  176.8 296.7 %reduce-scatter.2.cloned.1.call-start = ((), (), s32[]{:S(2)}) async-start(), calls=%async_computation.4 | async-start | bytes 5308416 | tf_op jit(solution)/shard_map/reduce_scatter | solution.py:27
  232.7 1.7 copy-start.4
  234.6 1.0 copy-start.5
  282.0 101.6 %copy-start = (f32[1152,512]{1,0:T(8,128)S(1)}, f32[1152,512]{1,0:T(8,128)}, u32[]{:S(2)}) copy-start(f32[1152,512]{1,0:T(8,128)} %all-reduce.5.cloned.1.call-done) | copy-start | bytes 7077892
  383.6 0.8 copy-start.6
  383.6 13.6 %slice-start = ((s8[5308416]{0:T(1024)(128)(4,1)}), s8[4194304]{0:T(1024)(128)(4,1)S(1)}, s32[]{:S(2)}) async-start(s8[5308416]{0:T(1024)(128)(4,1)} %bitcast.54), calls=%async_computation.6 | async-start | bytes 8388608
  386.8 4.7 copy-start.7
  388.4 8.8 %slice-start.1 = ((s8[5308416]{0:T(1024)(128)(4,1)}), s8[1114112]{0:T(1024)(128)(4,1)S(1)}, s32[]{:S(2)}) async-start(s8[5308416]{0:T(1024)(128)(4,1)} %bitcast.54), calls=%async_computation.7 | async-start | bytes 2228224
  392.2 5.0 copy-start.1
  420.3 53.2 %copy-start.8 = (u32[32]{0:T(128)S(1)}, u32[32]{0:T(128)}, u32[]{:S(2)}) copy-start(u32[32]{0:T(128)} %constant.172) | copy-start | bytes 388
  420.4 93.8 %copy-start.2 = (f32[128,1152]{1,0:T(8,128)S(1)}, f32[128,1152]{1,0:T(8,128)}, u32[]{:S(2)}) copy-start(f32[128,1152]{1,0:T(8,128)} %copy-done.1) | copy-start | bytes 1769476
  420.4 93.8 %all-gather.5.cloned.1.call-start = ((), (), s32[]{:S(2)}) async-start(), calls=%async_computation.5 | async-start | bytes 5308416 | tf_op jit(solution)/shard_map/all_gather | solution.py:34
  514.2 24.1 %copy-start.3 = (f32[512,2304]{1,0:T(8,128)S(1)}, f32[512,2304]{1,0:T(8,128)}, u32[]{:S(2)}) copy-start(f32[512,2304]{1,0:T(8,128)} %all-gather.5.cloned.1.call-done) | copy-start | bytes 14155780
Sparse Core Ops, SparseCore 0:
  9.9 41.4 all-gather.2
  74.4 94.6 all-reduce.4
  176.9 55.7 all-reduce.6
  420.5 53.0 reduce-scatter.1
  475.3 38.9 all-gather.4
where the time goes:
time: 574 us; the launch traced here: 566 us
  waiting for transfers between devices  260 us (45%)
  other arithmetic  128 us (22%)
  matrix products  118 us (21%)
  blocking collectives  23.8 us (4%)
  between operations  17.8 us (3%)
  local copies, waits for them, and re-layouts  17.7 us (3%)
    dot_general x5, matrix products, matmul(): jnp.dot(left, right, preferred_element_type=jnp.float32, precision=lax.Pr...  98.4 us
    psum x1, waiting for transfers between devices, per_device(): projected = lax.psum(partial_left, 'narrow')  94.7 us
    another operation x14, other arithmetic, orthonormal(): factor_lower = jnp.linalg.cholesky(gram_matrix)  83.1 us
    psum x1, waiting for transfers between devices, per_device(): gram_matrix = lax.psum(matmul(projected.T, projected), 'wide')  55.6 us
    reduce_scatter x1, waiting for transfers between devices, per_device(): lax.psum_scatter(matmul(columns.T, blended), 'wide', scatter_dimension=0,...  53.1 us
    all_gather x1, waiting for transfers between devices, per_device(): lax.all_gather(right_factor, 'wide', axis=0, tiled=True)  43.5 us
    another operation x3, other arithmetic, orthonormal(): jax.scipy.linalg.solve_triangular(factor_lower, projected.T, lower=True)  41.4 us
    another operation x12, local copies, waits for them, and re-layouts  13.7 us
  transfers between devices with their start and end apart: 5, of which 5 were waited for; matrix products, arithmetic and copies ran while one was open for 1% of the time, Pallas kernels for 0%

commit v1 on v0

--- a/solution.py
+++ b/solution.py
@@ -20,7 +20,11 @@
 def per_device(momentum, gradient, right_factor):
     blended = momentum + gradient.astype(jnp.float32)
     partial_left = matmul(blended, lax.all_gather(right_factor, "wide", axis=0, tiled=True).T)
-    projected = lax.psum(partial_left, "narrow")
+    projected = partial_left
+    for hop in (1, 2):
+        projected = projected + lax.ppermute(
+            projected, "narrow", [(dev, dev ^ hop) for dev in range(4)]
+        )
     gram_matrix = lax.psum(matmul(projected.T, projected), "wide")
     left_basis = orthonormal(projected, gram_matrix)
     columns = left_basis

time: 574 us -> 621 us (1.082)
  waiting for transfers between devices: 260 us -> 316 us
  matrix products: 118 us -> 111 us
    ppermute x0 -> x2, waiting for transfers between devices: none -> 154 us  [per_device(): lax.ppermute(projected, 'narrow', [(dev, dev ^ hop) for dev in range(4)])]
    psum x1 -> x0, waiting for transfers between devices: 94.7 us -> none  [per_device(): projected = lax.psum(partial_left, 'narrow')]
  transfers between devices with their start and end apart: 5 -> 6, of which waited for: 5 -> 6; matrix products, arithmetic and copies ran while one was open for 1% -> 1% of each run, Pallas kernels for 0% -> 0%
where the time goes in v1:
time: 621 us; the launch traced here: 613 us
  waiting for transfers between devices  316 us (51%)
  other arithmetic  127 us (20%)
  matrix products  111 us (18%)
  blocking collectives  23.8 us (4%)
  between operations  17.8 us (3%)
  local copies, waits for them, and re-layouts  13.3 us (2%)
    ppermute x2, waiting for transfers between devices, per_device(): lax.ppermute(projected, 'narrow', [(dev, dev ^ hop) for dev in range(4)])  154 us
    dot_general x5, matrix products, matmul(): jnp.dot(left, right, preferred_element_type=jnp.float32, precision=lax.Pr...  96.5 us
    another operation x14, other arithmetic, orthonormal(): factor_lower = jnp.linalg.cholesky(gram_matrix)  79 us
    reduce_scatter x1, waiting for transfers between devices, per_device(): lax.psum_scatter(matmul(columns.T, blended), 'wide', scatter_dimension=0,...  53.1 us
    psum x1, waiting for transfers between devices, per_device(): gram_matrix = lax.psum(matmul(projected.T, projected), 'wide')  53 us
    all_gather x1, waiting for transfers between devices, per_device(): lax.all_gather(right_factor, 'wide', axis=0, tiled=True)  43.5 us
    another operation x3, other arithmetic, orthonormal(): jax.scipy.linalg.solve_triangular(factor_lower, projected.T, lower=True)  40.3 us
  transfers between devices with their start and end apart: 6, of which 6 were waited for; matrix products, arithmetic and copies ran while one was open for 1% of the time, Pallas kernels for 0%

profile of v1, /device:TPU:0, one launch (start us, length us, event | category | flops | bytes accessed | tf_op | source)
XLA Modules:
  0.0 613.0 jit_solution(15405814856366141634)
XLA Ops:
  7.2 0.7 all-gather.3.cloned.1.call-update
  7.9 43.5 %all-gather.3.cloned.1.call-done = f32[512,2304]{1,0:T(8,128)} async-done(((f32[64,2304]{1,0:T(8,128)}), f32[512,2304]{1,0:T(8,128)}) %all-gather.3.cloned.1.call-update) | async-done | bytes 4718608 | tf_op jit(solution)/shard_map/all_gather | solution.py:22
  51.4 20.9 %fusion.3 = f32[1152,512]{1,0:T(8,128)S(1)} fusion(f32[512,2304]{1,0:T(8,128)} %all-gather.3.cloned.1.call-done, f32[1152,2304]{1,0:T(8,128)} %param.3, bf16[1152,2304]{1,0:T(8,128)(2,1)} %param.4), kind=kOutput, calls=%fused_computation.8 | convolution fusion | flops 16312762368 | bytes 23003136 | tf_op jit(solution)/shard_map/dot_general | solution.py:17
  72.3 1.6 collective-permute-start
  73.8 51.9 %collective-permute-done = f32[1152,512]{1,0:T(8,128)S(1)} collective-permute-done((f32[1152,512]{1,0:T(8,128)S(1)}, f32[1152,512]{1,0:T(8,128)S(1)}, u32[]{:S(2)}, u32[]{:S(2)}) %collective-permute-start) | collective-permute-done | bytes 2359328 | tf_op jit(solution)/shard_map/ppermute | solution.py:25
  125.7 0.5 add.63
  126.3 2.5 collective-permute-start.1
  128.8 101.7 %collective-permute-done.1 = f32[1152,512]{1,0:T(8,128)} collective-permute-done((f32[1152,512]{1,0:T(8,128)S(1)}, f32[1152,512]{1,0:T(8,128)}, u32[]{:S(2)}, u32[]{:S(2)}) %collective-permute-start.1) | collective-permute-done | bytes 2359328 | tf_op jit(solution)/shard_map/ppermute | solution.py:25
  230.5 7.8 %fusion.16 = f32[512,512]{0,1:T(8,128)} fusion(f32[1152,512]{1,0:T(8,128)S(1)} %add.63, f32[1152,512]{1,0:T(8,128)} %collective-permute-done.1), kind=kOutput, calls=%fused_computation.31 | convolution fusion | flops 3624468480 | bytes 5767168 | tf_op jit(solution)/shard_map/dot_general | solution.py:17
  238.3 0.3 reduce-scatter.2.cloned.1.call-start
  238.5 3.6 add_bitcast_fusion
  242.2 53.0 %all-reduce.4.cloned.1.call-done = f32[512,512]{0,1:T(8,128)} async-done(((f32[512,512]{0,1:T(8,128)}), f32[512,512]{0,1:T(8,128)}) %all-reduce.4.cloned.1.call-update) | async-done | bytes 1048592 | tf_op jit(solution)/shard_map/psum | solution.py:28
  295.1 1.6 copy.7
  296.8 0.2 fusion.15
  297.0 11.7 %cholesky.104 = f32[128,128]{1,0:T(8,128)S(1)} custom-call(f32[128,128]{1,0:T(8,128)S(1)} %cholesky.266), custom_call_target="Cholesky" | custom-call | tf_op jit(solution)/shard_map/jit(cholesky)/cholesky | solution.py:12
  308.8 9.8 %custom-call.31 = f32[1,128,128]{1,2,0:T(8,128)S(1)} custom-call(f32[1,128,128]{2,1,0:T(8,128)S(1)} %get-tuple-element.30), custom_call_target="InvertDiagBlocksLowerTriangular" | custom-call | tf_op jit(solution)/shard_map/jit(cholesky)/cholesky | solution.py:12
  318.6 0.1 cholesky.224
  318.7 0.3 constant_dynamic-update-slice_fusion.3
  319.0 0.3 convolution_subtract_fusion
  319.4 11.7 %cholesky.217 = f32[128,128]{1,0:T(8,128)S(1)} custom-call(f32[128,128]{1,0:T(8,128)S(1)} %cholesky.270), custom_call_target="Cholesky" | custom-call | tf_op jit(solution)/shard_map/jit(cholesky)/cholesky | solution.py:12
  331.1 10.2 %custom-call.32 = f32[1,128,128]{1,2,0:T(8,128)S(1)} custom-call(f32[1,128,128]{2,1,0:T(8,128)S(1)} %get-tuple-element.27), custom_call_target="InvertDiagBlocksLowerTriangular" | custom-call | tf_op jit(solution)/shard_map/jit(cholesky)/cholesky | solution.py:12
  341.3 0.3 convolution_dynamic-update-slice_fusion
  341.6 0.4 convolution_subtract_fusion.1
  342.0 11.7 %cholesky.238 = f32[128,128]{1,0:T(8,128)S(1)} custom-call(f32[128,128]{1,0:T(8,128)S(1)} %cholesky.275), custom_call_target="Cholesky" | custom-call | tf_op jit(solution)/shard_map/jit(cholesky)/cholesky | solution.py:12
  353.8 0.7 compare_reduce_fusion.1
  354.5 9.8 %custom-call.33 = f32[1,128,128]{1,2,0:T(8,128)S(1)} custom-call(f32[1,128,128]{2,1,0:T(8,128)S(1)} %get-tuple-element.24), custom_call_target="InvertDiagBlocksLowerTriangular" | custom-call | tf_op jit(solution)/shard_map/jit(cholesky)/cholesky | solution.py:12
  364.3 0.2 convolution_dynamic-update-slice_fusion.1
  364.5 0.4 convolution_subtract_fusion.2
  364.9 11.9 %cholesky.255 = f32[128,128]{1,0:T(8,128)S(1)} custom-call(f32[128,128]{1,0:T(8,128)S(1)} %convolution_subtract_fusion.2), custom_call_target="Cholesky" | custom-call | tf_op jit(solution)/shard_map/jit(cholesky)/cholesky | solution.py:12
  376.8 0.6 compare_reduce_fusion
  377.4 0.7 compare_reduce_fusion.2
  380.6 0.1 select_select_fusion
  380.8 10.9 %while.1 = (s32[]{:T(128)}, f32[512,512]{1,0:T(8,128)S(1)}, s32[4,2]{0,1:T(2,128)S(1)}, f32[4,128,128]{2,1,0:T(8,128)}, s32[]{:T(128)}) while((s32[]{:T(128)}, f32[512,512]{1,0:T(8,128)S(1)}, s32[4,2]{0,1:T(2,128)S(1)}, f32[4,128,128]{2,1,0:T(8,128)}, s32[]{:T(128)}) %tuple.32), condition=%wide.while_cond, body=%wide.while_body.sunk | while | flops 2 | bytes 132205 | solution.py:13
  380.8 0.1 constant_dynamic-slice_fusion.2
  380.9 0.6 fusion.50
  381.5 2.1 bitcast_dynamic-update-slice_fusion.2
  383.5 0.1 constant_dynamic-slice_fusion.2
  383.6 0.6 fusion.50
  384.2 2.1 bitcast_dynamic-update-slice_fusion.2
  386.3 0.1 constant_dynamic-slice_fusion.2
  386.3 0.6 fusion.50
  386.9 2.1 bitcast_dynamic-update-slice_fusion.2
  389.0 0.1 constant_dynamic-slice_fusion.2
  389.1 0.6 fusion.50
  389.7 2.1 bitcast_dynamic-update-slice_fusion.2
  391.7 40.2 %custom-call.34 = f32[4,128,128]{1,2,0:T(8,128)S(1)} custom-call(f32[4,128,128]{2,1,0:T(8,128)} %get-tuple-element.10), custom_call_target="InvertDiagBlocksLowerTriangular" | custom-call | tf_op jit(solution)/shard_map/jit(_solve_triangular)/triangular_solve | solution.py:13
  431.9 1.9 fusion.21
  433.8 1.1 fusion.31
  434.9 1.9 fusion.20
  436.8 2.0 fusion.11
  438.9 0.7 fusion.19
  439.6 3.9 fusion.5
  443.5 0.7 fusion.18
  444.3 23.1 %fusion.2 = f32[512,2304]{1,0:T(8,128)} fusion(f32[1152,2304]{1,0:T(8,128)} %param.3, bf16[1152,2304]{1,0:T(8,128)(2,1)S(1)} %bitcast.51, f32[128,1152]{1,0:T(8,128)S(1)} %fusion.18, f32[128,1152]{1,0:T(8,128)S(1)} %fusion.19, f32[128,1152]{1,0:T(8,128)S(1)} %fusion.20, f32[128,1152]{1,0:T(8,128)S(1)} %fusion.21), kind=kOutput, calls=%fused_computation.7 | convolution fusion | flops 16314531840 | bytes 23003136 | tf_op jit(solution)/shard_map/dot_general | solution.py:17
  467.5 53.1 %reduce-scatter.2.cloned.1.call-done = f32[64,2304]{1,0:T(8,128)} async-done(((f32[512,2304]{1,0:T(8,128)}), f32[64,2304]{1,0:T(8,128)}) %reduce-scatter.2.cloned.1.call-update) | async-done | bytes 589840 | tf_op jit(solution)/shard_map/reduce_scatter | solution.py:31
  520.6 0.6 dynamic-slice.3
  521.8 1.2 multiply_reduce_fusion
  523.0 11.7 %psum.15 = f32[64]{0:T(128)S(1)} all-reduce(f32[64]{0:T(128)S(1)} %multiply_reduce_fusion), channel_id=1, replica_groups=mesh['wide'=8,'narrow'=4] {'narrow'}, use_global_device_ids=true, to_apply=%region_11.12 | all-reduce | flops 64 | bytes 512 | tf_op jit(solution)/shard_map/psum | solution.py:34
  534.7 0.1 fusion.43
  534.8 12.1 %all-reduce.1 = f32[512]{0:T(512)S(1)} all-reduce(f32[512]{0:T(512)S(1)} %get-tuple-element.31), channel_id=1, replica_groups=mesh['wide'=8,'narrow'=4] {'wide'}, use_global_device_ids=true, to_apply=%add.1 | all-reduce | flops 512 | bytes 4096
  546.9 2.0 broadcast_divide_fusion
  548.9 12.3 %all-gather.5.cloned.1.call-done = f32[512,2304]{1,0:T(8,128)} async-done(((f32[64,2304]{1,0:T(8,128)}), f32[512,2304]{1,0:T(8,128)}) %all-gather.5.cloned.1.call-update) | async-done | bytes 4718608 | tf_op jit(solution)/shard_map/all_gather | solution.py:38
  561.3 24.1 %fusion = f32[1152,2304]{1,0:T(8,128)} fusion(f32[512,2304]{1,0:T(8,128)} %all-gather.5.cloned.1.call-done, f32[1152,2304]{1,0:T(8,128)} %param.3, bf16[1152,2304]{1,0:T(8,128)(2,1)} %param.4, f32[128,1152]{1,0:T(8,128)S(1)} %fusion.18, f32[128,1152]{1,0:T(8,128)S(1)} %fusion.19, f32[128,1152]{1,0:T(8,128)S(1)} %fusion.20, f32[128,1152]{1,0:T(8,128)S(1)} %fusion.21), kind=kOutput, calls=%fused_computation.3 | convolution fusion | flops 16319840256 | bytes 33619968 | tf_op jit(solution)/shard_map/dot_general | solution.py:17
  585.3 20.7 %convolution_convert_fusion = bf16[1152,2304]{1,0:T(8,128)(2,1)} fusion(f32[512,2304]{1,0:T(8,128)S(1)} %copy-done.1, f32[512]{0:T(512)S(1)} %all-reduce.1, f32[128,1152]{1,0:T(8,128)S(1)} %fusion.18, f32[128,1152]{1,0:T(8,128)S(1)} %fusion.19, f32[128,1152]{1,0:T(8,128)S(1)} %fusion.20, f32[128,1152]{1,0:T(8,128)S(1)} %fusion.21), kind=kOutput, calls=%fused_computation.4 | convolution fusion | flops 16313057280 | bytes 12388352 | tf_op jit(solution)/shard_map/dot_general | solution.py:17
  (36 shorter events, 0.4 us)
Async XLA Ops:
  7.2 44.2 %all-gather.3.cloned.1.call-start = ((), (), s32[]{:S(2)}) async-start(), calls=%async_computation.1 | async-start | bytes 5308416 | tf_op jit(solution)/shard_map/all_gather | solution.py:22
  7.9 287.2 %all-reduce.4.cloned.1.call-start = ((), (), s32[]{:S(2)}) async-start(), calls=%async_computation.2 | async-start | bytes 2097152 | tf_op jit(solution)/shard_map/psum | solution.py:28
  72.3 53.5 %collective-permute-start = (f32[1152,512]{1,0:T(8,128)S(1)}, f32[1152,512]{1,0:T(8,128)S(1)}, u32[]{:S(2)}, u32[]{:S(2)}) collective-permute-start(f32[1152,512]{1,0:T(8,128)S(1)} %fusion.3), channel_id=1, source_target_pairs={{0,1},{1,0},{2,3},{3,2},{4,5},{5,4},{6,7},{7,6},{8,9},{9,8},{10,11... | collective-permute-start | bytes 7077896 | tf_op jit(solution)/shard_map/ppermute | solution.py:25
  126.3 104.2 %collective-permute-start.1 = (f32[1152,512]{1,0:T(8,128)S(1)}, f32[1152,512]{1,0:T(8,128)}, u32[]{:S(2)}, u32[]{:S(2)}) collective-permute-start(f32[1152,512]{1,0:T(8,128)S(1)} %add.63), channel_id=1, source_target_pairs={{0,2},{1,3},{2,0},{3,1},{4,6},{5,7},{6,4},{7,5},{8,10},{9,11},{10,... | collective-permute-start | bytes 7077896 | tf_op jit(solution)/shard_map/ppermute | solution.py:25
  238.3 282.3 %reduce-scatter.2.cloned.1.call-start = ((), (), s32[]{:S(2)}) async-start(), calls=%async_computation.3 | async-start | bytes 5308416 | tf_op jit(solution)/shard_map/reduce_scatter | solution.py:31
  295.1 1.7 copy-start.2
  380.8 63.5 %slice-start = ((s8[5308416]{0:T(1024)(128)(4,1)}), s8[1114112]{0:T(1024)(128)(4,1)S(1)}, s32[]{:S(2)}) async-start(s8[5308416]{0:T(1024)(128)(4,1)} %bitcast.50), calls=%async_computation.5 | async-start | bytes 2228224
  391.7 45.1 %copy-start.3 = (f32[512,512]{1,0:T(8,128)}, f32[512,512]{1,0:T(8,128)S(1)}, u32[]{:S(2)}) copy-start(f32[512,512]{1,0:T(8,128)S(1)} %get-tuple-element.95) | copy-start | bytes 3145732
  431.9 1.9 copy-start.4
  433.8 5.1 copy-start
  434.9 3.9 copy-start.5
  436.8 7.5 %slice-start.1 = ((s8[5308416]{0:T(1024)(128)(4,1)}), s8[4194304]{0:T(1024)(128)(4,1)S(1)}, s32[]{:S(2)}) async-start(s8[5308416]{0:T(1024)(128)(4,1)} %bitcast.50), calls=%async_computation.6 | async-start | bytes 8388608
  467.4 53.2 %copy-start.6 = (u32[32]{0:T(128)S(1)}, u32[32]{0:T(128)}, u32[]{:S(2)}) copy-start(u32[32]{0:T(128)} %constant.172) | copy-start | bytes 388
  467.4 93.8 %all-gather.5.cloned.1.call-start = ((), (), s32[]{:S(2)}) async-start(), calls=%async_computation.4 | async-start | bytes 5308416 | tf_op jit(solution)/shard_map/all_gather | solution.py:38
  561.3 24.1 %copy-start.1 = (f32[512,2304]{1,0:T(8,128)S(1)}, f32[512,2304]{1,0:T(8,128)}, u32[]{:S(2)}) copy-start(f32[512,2304]{1,0:T(8,128)} %all-gather.5.cloned.1.call-done) | copy-start | bytes 14155780
Sparse Core Ops, SparseCore 0:
  9.9 41.4 all-gather.2
  238.4 56.6 all-reduce.3
  467.5 52.9 reduce-scatter.1
  522.3 38.9 all-gather.4
